TPU v7x, 16 devices: a whole 2x2x2 slice. The times are simulated.
16 devices in a mesh: dp: 2 (over z), sp: 8 (over y, x, core).
Axes of the slice: x: 2, y: 2, z: 2, core: 2. Of those that a mesh axis runs over, the one named last changes fastest.
Arguments:
- feat_p3: bfloat16 [32, 256, 80, 256], P('dp', 'sp'), parts along dimension 0
- feat_p4: bfloat16 [32, 128, 40, 256], P('dp', 'sp'), parts along dimension 0
- feat_p5: bfloat16 [32, 64, 20, 256], P('dp', 'sp'), parts along dimension 0
- feat_p6: bfloat16 [32, 32, 10, 256], P('dp', 'sp'), parts along dimension 0
- feat_p7: bfloat16 [32, 16, 5, 256], P('dp', 'sp'), parts along dimension 0
- fuse_two: float32 [5, 2], replicated
- fuse_three: float32 [3, 3], replicated
- dw_filter: bfloat16 [8, 3, 3, 256], replicated
- pw_weight: bfloat16 [8, 256, 256], replicated
- bn_scale: float32 [8, 256], replicated
- bn_bias: float32 [8, 256], replicated
Outputs:
- output 1: bfloat16 [32, 256, 80, 256], P('dp', 'sp'), parts along dimension 0
- output 2: bfloat16 [32, 128, 40, 256], P('dp', 'sp'), parts along dimension 0
- output 3: bfloat16 [32, 64, 20, 256], P('dp', 'sp'), parts along dimension 0
- output 4: bfloat16 [32, 32, 10, 256], P('dp', 'sp'), parts along dimension 0
- output 5: bfloat16 [32, 16, 5, 256], P('dp', 'sp'), parts along dimension 0
There are 2 independent parts. A program takes and returns all parts, laid end to end along the dimension named above; an argument that names none is the same for every part.
All inputs are finite; a program needn't handle non-finite values.
Results may differ from a plain program's by a relative error of at most 0.00876237.
Values are sent between devices in bfloat16 or wider.
A program may use at most 1 GiB of HBM per device.

v0:
```python
import functools

import jax
import jax.numpy as jnp
from jax import lax
from jax.experimental import pallas as pl
from jax.experimental.pallas import tpu as pltpu
from jax.sharding import PartitionSpec as P

f32, bf16 = jnp.float32, jnp.bfloat16
FUSE_EPS = 1e-4
B, C, H = 16, 256, 128
G = N = 4
LV = (4, 5, 6, 7)
LOW = LV[1:]
TOP, END = 4, 7
TWO, THREE = range(2), range(3)
ROWS = {3: 32, 4: 16, 5: 8, 6: 4, 7: 2}
COLS = {3: 80, 4: 40, 5: 20, 6: 10, 7: 5}
PADC = {3: 80, 4: 40, 5: 24, 6: 16, 7: 8}
TILE = 8
MESH = pl.DeviceIdType.MESH
NEG = -jnp.inf
MIB = 2 ** 20


def groups(fn):
    def body(g, _):
        fn(g)
        return g
    lax.fori_loop(0, G, body, G)


def loop(n, unroll=1):
    def run(fn):
        def body(i, _):
            fn(i)
            return i
        lax.fori_loop(0, n, body, n, unroll=unroll)
    return run


def swish(h):
    return h + h * jnp.tanh(h)


def halves(v):
    return v[:, :H], v[:, H:]


def join(v):
    return jnp.concatenate(v, axis=1)


def half(c):
    return slice(c * H, c * H + H)


def cols(W, d=0):
    return slice(TILE + d, TILE + d + W)


def coefs(two, three, k):
    w = [two[i, min(k, 4)] for i in TWO] if k < 4 or k == 7 else [three[k - 4, i] for i in THREE]
    w = [jnp.maximum(x, 0.0) for x in w]
    total = jnp.full((1, C), sum(w[1:], w[0]) + FUSE_EPS, f32)
    return [jnp.full((1, C), 0.5 * x, f32) / total for x in w]


def widen(dw_ref, DW):
    for ky in THREE:
        for kx in THREE:
            DW[3 * ky + kx] = dw_ref[ky, kx].astype(f32)


def tap(DW, k, ky, kx, c):
    return DW[3 * ky + kx, k:k + 1, half(c)]


def zero_edges(S, W):
    S[..., :TILE, :] = jnp.zeros(S.shape[:-2] + (TILE, H), f32)
    S[..., TILE + W:, :] = jnp.zeros(S.shape[:-2] + (S.shape[-2] - TILE - W, H), f32)


def expand(U, v, wc):
    for c, h in enumerate(halves(v)):
        for d in TWO:
            U[c, pl.ds(d, wc, stride=2), :] = h
    return join([U[0], U[1]])


def put_s(S, ib, s, W, h):
    v = swish(h).astype(bf16).astype(f32)
    for c, x in enumerate(halves(v)):
        S[ib, c, s, cols(W), :] = x


def conv_row(S, ib, o, W, DW, k):
    out = []
    for c in TWO:
        acc = None
        for ky in THREE:
            for kx in THREE:
                t = S[ib, c, o + ky, cols(W, kx - 1), :] * tap(DW, k, ky, kx, c)
                acc = t if acc is None else acc + t
        out.append(acc)
    return join(out).astype(bf16)


def conv_rows(S, D, rows, level, k, wts, put):
    DW, pw_ref, sc_ref, bi_ref = wts
    W, wp = COLS[level], PADC[level]
    for i, (ib, o) in enumerate(rows):
        D[i * wp:i * wp + W, :] = conv_row(S, ib, o, W, DW, k)
    m = len(rows) * wp
    r = jnp.dot(D[:m], pw_ref[k], preferred_element_type=f32)
    r = (r * sc_ref[k:k + 1] + bi_ref[k:k + 1]).astype(bf16)
    for i, (ib, o) in enumerate(rows):
        put(ib, o, r[i * wp:i * wp + W])


def hmax(PV, v, W):
    out = []
    for c, x in enumerate(halves(v.astype(f32))):
        PV[c, :W, :] = x
        a, b, d = [PV[c, pl.ds(i, W // 2, stride=2), :] for i in THREE]
        out.append(jnp.maximum(jnp.maximum(a, b), d))
    return join(out).astype(bf16)


def barrier_signal(me, last):
    sem = pltpu.get_barrier_semaphore()
    for cond, d in ((me > 0, -1), (me < last, 1)):
        @pl.when(cond)
        def _(d=d):
            pl.semaphore_signal(sem, inc=1, device_id={'sp': me + d}, device_id_type=MESH)


def barrier_wait(me, last):
    sem = pltpu.get_barrier_semaphore()
    inner = (me > 0) & (me < last)

    @pl.when(inner)
    def _():
        pl.semaphore_wait(sem, 2)

    @pl.when(jnp.logical_not(inner))
    def _():
        pl.semaphore_wait(sem, 1)


def remote(src, dst, ss, rs, dev):
    return pltpu.make_async_remote_copy(src_ref=src, dst_ref=dst, send_sem=ss, recv_sem=rs, device_id={'sp': dev}, device_id_type=MESH)


def shape(l, r):
    return (B, r, COLS[l], C)


def flipped(l):
    return (B, COLS[l], ROWS[l], C)


def vm(s, t=bf16):
    return pltpu.VMEM(s, t)


DMA = pltpu.SemaphoreType.DMA
ANY = pl.BlockSpec(memory_space=pl.ANY)
VMEM = pl.BlockSpec(memory_space=pltpu.VMEM)
SMEM = pl.BlockSpec(memory_space=pltpu.SMEM)


def struct(s):
    return jax.ShapeDtypeStruct(s, bf16)


def splitter(refs):
    it = iter(refs)

    def take(n):
        return [next(it) for _ in range(n)]
    return take


EXT = {4: 2, 5: 2, 6: 2, 7: 1}
TD = (4, 5, 6)
SLOTS = {4: 1, 5: 1, 6: 4, 7: 4}


def top_down(*refs, n_dev):
    take = splitter(refs)
    two, three, p3, p4 = take(4)
    Q = dict(zip(LOW, take(3)))
    dw_ref, pw_ref, sc_ref, bi_ref = take(4)
    Th = dict(zip(TD, take(3)))
    h3, = take(1)
    X = dict(zip(LV, take(4)))
    E, T = dict(zip(LV, take(4))), dict(zip(TD, take(3)))
    S, U, F = dict(zip(TD, take(3))), dict(zip(TD, take(3))), dict(zip(LOW, take(3)))
    D, Z, DW, ls, os, xs, s_up, r_up, s_dn, r_dn, s3, r3, zs = take(13)
    me = lax.axis_index('sp')
    last = n_dev - 1
    wts = (DW, pw_ref, sc_ref, bi_ref)
    FINE_FIRST = (7, 6, 5, 4)

    def sl(g):
        return pl.ds(g * N, N)

    def load(g):
        return pltpu.make_async_copy(p4.at[sl(g)], E[4].at[sl(g), pl.ds(EXT[4], ROWS[4])], ls.at[g])

    def src(l, g, r):
        return p4.at[sl(g), pl.ds(r, EXT[l])] if l == TOP else E[l].at[sl(g), pl.ds(EXT[l] + r, EXT[l])]

    def up(l, g):
        e = EXT[l]
        return remote(src(l, g, 0), E[l].at[sl(g), pl.ds(e + ROWS[l], e)], s_up.at[l - TOP, g], r_up.at[l - TOP, g], me - 1)

    def dn(l, g):
        e = EXT[l]
        return remote(src(l, g, ROWS[l] - e), E[l].at[sl(g), pl.ds(0, e)], s_dn.at[l - TOP, g], r_dn.at[l - TOP, g], me + 1)

    up3 = remote(p3.at[:, pl.ds(0, 1)], h3.at[:, pl.ds(1, 1)], s3.at[0], r3.at[0], me - 1)
    dn3 = remote(p3.at[:, pl.ds(ROWS[3] - 1, 1)], h3.at[:, pl.ds(0, 1)], s3.at[1], r3.at[1], me + 1)

    barrier_signal(me, last)

    @groups
    def _(g):
        load(g).start()

    for l in FINE_FIRST[:-1]:
        W, R, st = COLS[l], ROWS[l], COLS[l] + 1

        @loop(B // 2)
        def _(i):
            for d in TWO:
                b = 2 * i + d
                for w in range(W):
                    for c, v in enumerate(halves(Q[l][b, w].astype(f32))):
                        F[l][d, c, pl.ds(w, R, stride=st), :] = v
                for r in range(R):
                    E[l][b, EXT[l] + r] = join([F[l][d, c, r * st:r * st + W, :] for c in TWO]).astype(bf16)
    widen(dw_ref, DW)
    for l in TD:
        zero_edges(S[l], COLS[l])
    Z[...] = jnp.zeros(Z.shape, bf16)
    edge = [pltpu.make_async_copy(Z, h3.at[:, pl.ds(i, 1)], zs) for i in TWO]

    @pl.when(me == 0)
    def _():
        edge[0].start()
        for l in LV:
            E[l][:, :EXT[l]] = jnp.zeros(shape(l, EXT[l]), bf16)

    @pl.when(me == last)
    def _():
        edge[1].start()
        for l in LV:
            E[l][:, EXT[l] + ROWS[l]:] = jnp.zeros(shape(l, EXT[l]), bf16)

    barrier_wait(me, last)
    for cond, cp, big in ((me > 0, up, up3), (me < last, dn, dn3)):
        @pl.when(cond)
        def _(cp=cp, big=big):
            @groups
            def _(g):
                for l in FINE_FIRST:
                    cp(l, g).start()
            big.start()

    def node(l, g):
        k = 6 - l
        W, wc, R = COLS[l], COLS[l + 1], ROWS[l]
        a1, a2 = coefs(two, three, k)
        coarse = E[7] if l == 6 else T[l + 1]
        nb = SLOTS[l]

        def fill(b, ib, j, u):
            x = expand(U[l].at[u], coarse[b, j].astype(f32) * a2, wc)
            for d in TWO:
                put_s(S[l], ib, 2 * j + d, W, E[l][b, 2 * j + d].astype(f32) * a1 + x)

        @loop(N // nb)
        def _(i):
            b0 = g * N + i * nb

            def put(ib, o, v):
                T[l][b0 + ib, o] = v
            if l == TOP:
                @loop((R + 4) // 4)
                def _(j):
                    for u in TWO:
                        fill(b0, 0, 2 * j + u, u)

                @loop(3)
                def _(q):
                    conv_rows(S[l], D, [(0, q * 6 + y) for y in range(6)], l, k, wts, put)
            else:
                for ib in range(nb):
                    for j in range((R + 4) // 2):
                        fill(b0 + ib, ib, j, (ib + j) % 2)
                conv_rows(S[l], D, [(ib, o) for ib in range(nb) for o in range(R + 2)], l, k, wts, put)

        for cond, o in ((me == 0, 0), (me == last, R + 1)):
            @pl.when(cond)
            def _(o=o):
                T[l][sl(g), o:o + 1] = jnp.zeros((N, 1, W, C), bf16)

    def out(l, g):
        return pltpu.make_async_copy(T[l].at[sl(g)], Th[l].at[sl(g)], os.at[l - TOP, g])

    def xout(l):
        return pltpu.make_async_copy(E[l].at[:, pl.ds(EXT[l] - 1, 1)], X[l], xs.at[l - 4])

    def arrive(l, g):
        @pl.when(me > 0)
        def _():
            dn(l, g).wait_recv()

        @pl.when(me < last)
        def _():
            up(l, g).wait_recv()

    @groups
    def _(g):
        arrive(7, g)
        for l in (6, 5, 4):
            if l == TOP:
                load(g).wait()
            arrive(l, g)
            node(l, g)
            out(l, g).start()
    for l in LV:
        xout(l).start()

    for cond, cp, sent, got in ((me > 0, up, up3, dn3), (me < last, dn, dn3, up3)):
        @pl.when(cond)
        def _(cp=cp, sent=sent, got=got):
            @groups
            def _(g):
                for l in LV:
                    cp(l, g).wait_send()
            sent.wait_send()
            got.wait_recv()

    for cond, e in ((me == 0, edge[0]), (me == last, edge[1])):
        @pl.when(cond)
        def _(e=e):
            e.wait()
    for l in LV:
        xout(l).wait()

    @groups
    def _(g):
        for l in TD:
            out(l, g).wait()


def call_top_down(n_dev, two, three, p3, p4, qs, wts):
    scratch = [vm(shape(l, ROWS[l] + 2 * EXT[l])) for l in LV] + [vm(shape(l, ROWS[l] + 2)) for l in TD]
    scratch += [vm((SLOTS[l], 2, ROWS[l] + 4, PADC[l] + 2 * TILE, H), f32) for l in TD]
    scratch += [vm((2, 2, COLS[l], H), f32) for l in TD]
    scratch += [vm((2, 2, TILE * -(-ROWS[l] * (COLS[l] + 1) // TILE), H), f32) for l in LOW]
    scratch += [vm((24 * 16 + TILE, C)), vm(shape(3, 1)), vm((9, TILE, C), f32)]
    scratch += [DMA((G,)), DMA((3, G)), DMA((4,))] + [DMA((4, G))] * 4 + [DMA((2,))] * 2 + [DMA]
    return pl.pallas_call(
        functools.partial(top_down, n_dev=n_dev),
        out_shape=[struct(shape(l, ROWS[l] + 2)) for l in TD] + [struct(shape(3, 2))] + [struct(shape(l, 1)) for l in LV],
        in_specs=[SMEM] * 2 + [ANY] * 2 + [VMEM] * 7,
        out_specs=[ANY] * 8,
        scratch_shapes=scratch,
        compiler_params=pltpu.CompilerParams(collective_id=0, has_side_effects=True, vmem_limit_bytes=60 * MIB),
    )(two, three, p3, p4, *qs, *wts)


R3, W3 = ROWS[3], COLS[3]
RC3, WC3 = ROWS[4], COLS[4]
PB = 4
NB = RC3 // PB
K3 = 3 * C


def fine(two, three, p_ref, ph_ref, t_ref, dw_ref, pw_ref, sc_ref, bi_ref, o_ref, d_ref, h_ref, S0, S1, U, X0, X1, D0, D1, PV, WD, DW):
    R, W, RC, WC = R3, W3, RC3, WC3
    Xb, Db = (X0, X1), (D0, D1)
    a1, a2 = coefs(two, three, 3)
    b = pl.program_id(0)

    @pl.when(b == 0)
    def _():
        widen(dw_ref, DW)
        zero_edges(S0, W)
        zero_edges(S1, W)
        PV[:, W:, :] = jnp.full((2, TILE, H), NEG, f32)
        eye = lax.broadcasted_iota(jnp.int32, (H, H), 0) == lax.broadcasted_iota(jnp.int32, (H, H), 1)
        for c in TWO:
            for kx in THREE:
                for pi in TWO:
                    for po in TWO:
                        v = jnp.where(eye, tap(DW, 3, 1 + pi - po, kx, c), 0.0)
                        r0 = kx * C + pi * H
                        WD[c, r0:r0 + H, half(po)] = v.astype(bf16)

    def p1(S, tj, rows, u):
        x = expand(U.at[u], t_ref[0, tj + 1].astype(f32) * a2, WC)
        for v, si in rows:
            put_s(S, 0, si, W, v.astype(f32) * a1 + x)

    def borders(S):
        p1(S, -1, [(ph_ref[0, 0], 0)], 0)
        p1(S, RC, [(ph_ref[0, 1], R + 1)], 1)

    def act(S, k):
        for t in range(PB):
            tj = k * PB + t
            p1(S, tj, [(p_ref[0, 2 * tj + d], 2 * tj + d + 1) for d in TWO], t % 2)

    def gather(S, X, k):
        for c in TWO:
            for p in range(PB):
                for kx in THREE:
                    X[c, p * W:(p + 1) * W, kx * C:kx * C + C] = join(
                        [S[0, c, 2 * (k * PB + p) + 1 + par, cols(W, kx - 1), :] for par in TWO]).astype(bf16)

    def conv(S, X, D, k):
        for c in TWO:
            r = jnp.dot(X[c, :PB * W], WD[c], preferred_element_type=f32)
            for p in range(PB):
                for par in TWO:
                    si = 2 * (k * PB + p) + 3 * par
                    q = r[p * W:(p + 1) * W, half(par)]
                    for kx in THREE:
                        q = q + S[0, c, si, cols(W, kx - 1), :] * tap(DW, 3, 2 * par, kx, c)
                    y = 2 * p + par
                    D[y * W:(y + 1) * W, half(c)] = q.astype(bf16)

    def point(D, k):
        o = jnp.dot(D[:2 * PB * W], pw_ref[3], preferred_element_type=f32)
        o = (o * sc_ref[3:4] + bi_ref[3:4]).astype(bf16)
        for y in range(2 * PB):
            o_ref[0, 2 * PB * k + y] = o[y * W:(y + 1) * W]

    def step(Sn, Sp):
        if Sn is not None:
            borders(Sn)
        gather(Sp, Xb[0], 0)

        @loop(NB // 2)
        def _(kk):
            for u in TWO:
                k = 2 * kk + u
                point(Db[1 - u], jnp.maximum(k - 1, 0))
                conv(Sp, Xb[u], Db[u], k)
                gather(Sp, Xb[1 - u], jnp.minimum(k + 1, NB - 1))
                if Sn is not None:
                    act(Sn, k)
        point(Db[1], NB - 1)

    @pl.when(b == 0)
    def _():
        borders(S0)

        @loop(NB)
        def _(k):
            act(S0, k)

    inner = (b > 0) & (b < B)

    @pl.when(inner & (b % 2 == 0))
    def _():
        step(S0, S1)

    @pl.when(inner & (b % 2 == 1))
    def _():
        step(S1, S0)

    @pl.when(b == B)
    def _():
        step(None, S1)

    @pl.when(b > 0)
    def _():
        h_ref[0, 0] = hmax(PV, o_ref[0, 0], W)

        @loop(RC, unroll=2)
        def _(r):
            rn = jnp.minimum(2 * r + 2, R - 1)
            d_ref[0, r] = hmax(PV, jnp.maximum(jnp.maximum(o_ref[0, 2 * r], o_ref[0, 2 * r + 1]), o_ref[0, rn]), W)


def call_fine(two, three, p, ph, t, wts):
    def block(s, late=False):
        return pl.BlockSpec((1,) + s[1:], lambda b: (jnp.maximum(b - 1, 0) if late else jnp.minimum(b, B - 1), 0, 0, 0))
    full = [pl.BlockSpec(a.shape, lambda b, n=a.ndim: (0,) * n) for a in wts]
    outs = [shape(3, R3), shape(4, RC3), shape(4, 1)]
    S = vm((1, 2, R3 + 2, W3 + 2 * TILE, H), f32)
    X = vm((2, PB * W3 + TILE, K3))
    D = vm((2 * PB * W3 + TILE, C))
    return pl.pallas_call(
        fine, grid=(B + 1,),
        out_shape=[struct(s) for s in outs],
        in_specs=[SMEM] * 2 + [block(a.shape) for a in (p, ph, t)] + full,
        out_specs=[block(s, True) for s in outs],
        scratch_shapes=[S, S, vm((2, 2, W3, H), f32), X, X, D, D, vm((2, W3 + TILE, H), f32), vm((2, K3, C)), vm((9, TILE, C), f32)],
        compiler_params=pltpu.CompilerParams(vmem_limit_bytes=60 * MIB),
    )(two, three, p, ph, t, *wts)


def bottom_up(*refs, n_dev):
    take = splitter(refs)
    two, three, p4 = take(3)
    Ph = {4: p4, **dict(zip(LOW, take(3)))}
    Xh, Th = dict(zip(LV, take(4))), dict(zip(TD, take(3)))
    d4, h4, dw_ref, pw_ref, sc_ref, bi_ref = take(6)
    Oh = dict(zip(LV, take(4)))
    Pv, Tv, Dv, Ov = dict(zip(LV, take(4))), dict(zip(TD, take(3))), dict(zip(LV, take(4))), dict(zip(LV, take(4)))
    UP, UR, DR, S = [dict(zip(LV, take(4))) for _ in range(4)]
    V = dict(zip(TD, take(3)))
    F = dict(zip(LOW, take(3)))
    D, DW, ls, os, s_up, r_up, s_dn, r_dn = take(8)
    me = lax.axis_index('sp')
    last = n_dev - 1
    wts = (DW, pw_ref, sc_ref, bi_ref)

    def sl(g):
        return pl.ds(g * N, N)

    def loads(l, g):
        q = sl(g)
        pairs = [(Xh[l].at[q], Pv[l].at[q, pl.ds(0, 1)])]
        if l == TOP:
            pairs += [(p4.at[q], Pv[4].at[q, pl.ds(1, ROWS[4])]), (d4.at[q], Dv[4].at[q]), (h4.at[q], UP[4].at[q, pl.ds(0, 1)])]
        if l < END:
            pairs += [(Th[l].at[q], Tv[l].at[q])]
        return [pltpu.make_async_copy(a, b, ls.at[l - TOP, g, i]) for i, (a, b) in enumerate(pairs)]

    def up(l, g):
        return remote(UP[l].at[sl(g)], UR[l].at[sl(g)], s_up.at[l - TOP, g], r_up.at[l - TOP, g], me - 1)

    def dn(l, g):
        return remote(Dv[l].at[sl(g), pl.ds(ROWS[l] - 1, 1)], DR[l].at[sl(g)], s_dn.at[l - TOP, g], r_dn.at[l - TOP, g], me + 1)

    def send(l, g):
        @pl.when(me > 0)
        def _():
            up(l, g).start()

        @pl.when(me < last)
        def _():
            dn(l, g).start()

    def arrive(l, g):
        @pl.when(me < last)
        def _():
            up(l, g).wait_recv()

        @pl.when(me > 0)
        def _():
            dn(l, g).wait_recv()

    CF = {l: coefs(two, three, l) for l in LV}

    def fuse(l, b, r, d):
        a = CF[l]
        h = Pv[l][b, r + 1].astype(f32) * a[0] + d.astype(f32) * a[-1]
        if l < END:
            h = h + Tv[l][b, r + 1].astype(f32) * a[1]
        return h

    def first(l, b):
        UP[l][b, 1] = swish(fuse(l, b, 0, Dv[l][b, 0])).astype(bf16)

    barrier_signal(me, last)

    @groups
    def _(g):
        for l in LV:
            for c in loads(l, g):
                c.start()
    widen(dw_ref, DW)
    for l in LV:
        zero_edges(S[l], COLS[l])
        if l < END:
            V[l][:, COLS[l]:COLS[l] + TILE, :] = jnp.full((2, TILE, H), NEG, f32)

    @pl.when(me == last)
    def _():
        for l in LV:
            UR[l][:, :1] = jnp.full(shape(l, 1), NEG, bf16)
            UR[l][:, 1:] = jnp.zeros(shape(l, 1), bf16)

    @pl.when(me == 0)
    def _():
        for l in LV:
            DR[l][...] = jnp.zeros(shape(l, 1), bf16)

    barrier_wait(me, last)

    @groups
    def _(g):
        for c in loads(4, g):
            c.wait()

        @loop(N)
        def _(i):
            first(4, g * N + i)
        send(4, g)

    for l in LOW:
        W, R, st = COLS[l], ROWS[l], COLS[l] + 1

        @loop(B // 2)
        def _(i):
            for d in TWO:
                b = 2 * i + d
                for w in range(W):
                    for c, v in enumerate(halves(Ph[l][b, w].astype(f32))):
                        F[l][d, c, pl.ds(w, R, stride=st), :] = v
                for r in range(R):
                    Pv[l][b, 1 + r] = join([F[l][d, c, r * st:r * st + W, :] for c in TWO]).astype(bf16)

    def node(l, g):
        W, R = COLS[l], ROWS[l]
        nb = SLOTS[l]

        def borders(b, ib):
            put_s(S[l], ib, 0, W, fuse(l, b, -1, jnp.maximum(DR[l][b, 0], UP[l][b, 0])))
            put_s(S[l], ib, R, W, fuse(l, b, R - 1, jnp.maximum(Dv[l][b, R - 1], UR[l][b, 0])))
            for c, v in enumerate(halves(UR[l][b, 1].astype(f32))):
                S[l][ib, c, R + 1, cols(W), :] = v

            @pl.when(me == 0)
            def _():
                S[l][ib, :, 0, cols(W), :] = jnp.zeros((2, W, H), f32)

        def pools(b):
            n = R // 2

            def row(r):
                return Ov[l][b, r]
            UP[l + 1][b, 0] = hmax(V[l], row(0), W)

            def pooled(r, inner):
                m = jnp.maximum(row(2 * r), row(2 * r + 1))
                if inner:
                    m = jnp.maximum(m, row(2 * r + 2))
                Dv[l + 1][b, r] = hmax(V[l], m, W)
            if l == TOP:
                @loop(n - 1)
                def _(r):
                    pooled(r, True)
            else:
                for r in range(n - 1):
                    pooled(r, True)
            pooled(n - 1, False)
            first(l + 1, b)

        @loop(N // nb)
        def _(i):
            b0 = g * N + i * nb
            for ib in range(nb):
                borders(b0 + ib, ib)

            def put(ib, o, v):
                Ov[l][b0 + ib, o] = v
            if l == TOP:
                @loop((R - 1) // 3)
                def _(r):
                    for y in THREE:
                        put_s(S[l], 0, 3 * r + y + 1, W, fuse(l, b0, 3 * r + y, Dv[l][b0, 3 * r + y]))

                @loop(R // 4)
                def _(q):
                    conv_rows(S[l], D, [(0, q * 4 + y) for y in range(4)], l, l, wts, put)
            else:
                for ib in range(nb):
                    for r in range(R - 1):
                        put_s(S[l], ib, r + 1, W, fuse(l, b0 + ib, r, Dv[l][b0 + ib, r]))
                conv_rows(S[l], D, [(ib, o) for ib in range(nb) for o in range(R)], l, l, wts, put)
            if l < END:
                for ib in range(nb):
                    pools(b0 + ib)

    def out(l, g):
        return pltpu.make_async_copy(Ov[l].at[sl(g)], Oh[l].at[sl(g)], os.at[l - TOP, g])

    @loop(G + 3)
    def _(t):
        for l in LV:
            g = t - (l - 4)

            @pl.when((g >= 0) & (g < G))
            def _(l=l, g=g):
                if l < END:
                    for c in loads(l + 1, g):
                        c.wait()
                arrive(l, g)
                node(l, g)
                if l < END:
                    send(l + 1, g)
                out(l, g).start()

    for cond, cp in ((me > 0, up), (me < last, dn)):
        @pl.when(cond)
        def _(cp=cp):
            @groups
            def _(g):
                for l in LV:
                    cp(l, g).wait_send()

    @groups
    def _(g):
        for l in LV:
            out(l, g).wait()


def call_bottom_up(n_dev, two, three, p4, qs, xs, ts, d4, h4, wts):
    scratch = [vm(shape(l, ROWS[l] + 1)) for l in LV] + [vm(shape(l, ROWS[l] + 2)) for l in TD]
    scratch += [vm(shape(l, ROWS[l])) for l in LV] * 2 + [vm(shape(l, 2)) for l in LV] * 2 + [vm(shape(l, 1)) for l in LV]
    scratch += [vm((SLOTS[l], 2, ROWS[l] + 2, PADC[l] + 2 * TILE, H), f32) for l in LV] + [vm((2, PADC[l] + TILE, H), f32) for l in TD]
    scratch += [vm((2, 2, TILE * -(-ROWS[l] * (COLS[l] + 1) // TILE), H), f32) for l in LOW]
    scratch += [vm((24 * 16 + TILE, C)), vm((9, TILE, C), f32), DMA((4, G, 5))] + [DMA((4, G))] * 5
    return pl.pallas_call(
        functools.partial(bottom_up, n_dev=n_dev),
        out_shape=[struct(shape(l, ROWS[l])) for l in LV],
        in_specs=[SMEM] * 2 + [ANY] + [VMEM] * 3 + [ANY] * 9 + [VMEM] * 4,
        out_specs=[ANY] * 4,
        scratch_shapes=scratch,
        compiler_params=pltpu.CompilerParams(collective_id=1, has_side_effects=True, vmem_limit_bytes=62 * MIB),
    )(two, three, p4, *qs, *xs, *ts, d4, h4, *wts)


def finish(i4, i5, i6, i7, o4, o5, o6, o7, buf, F5, F6, F7, si, so):
    def cin(g):
        return pltpu.make_async_copy(i4.at[pl.ds(g * N, N)], buf.at[pl.ds(g * N, N)], si.at[g])

    def cout(g):
        return pltpu.make_async_copy(buf.at[pl.ds(g * N, N)], o4.at[pl.ds(g * N, N)], so.at[g])

    for g in range(G):
        cin(g).start()
    for g, (l, src, dst, F) in enumerate(((6, i6, o6, F6), (7, i7, o7, F7), (5, i5, o5, F5))):
        W, R, st = COLS[l], ROWS[l], COLS[l] + 1

        @loop(B // 2)
        def _(i):
            for d in TWO:
                b = 2 * i + d
                for r in range(R):
                    for c, v in enumerate(halves(src[b, r].astype(f32))):
                        F[d, c, r * st:r * st + W, :] = v
                for w in range(W):
                    dst[b, w] = join([F[d, c, pl.ds(w, R, stride=st), :] for c in TWO]).astype(bf16)
        cin(g).wait()
        cout(g).start()
    cin(G - 1).wait()
    cout(G - 1).start()
    for g in range(G):
        cout(g).wait()


def call_finish(ins):
    return pl.pallas_call(
        finish,
        out_shape=[struct(shape(4, ROWS[4]))] + [struct(flipped(l)) for l in LOW],
        in_specs=[ANY] + [VMEM] * 3,
        out_specs=[ANY] + [VMEM] * 3,
        scratch_shapes=[vm(shape(4, ROWS[4]))] + [vm((2, 2, TILE * -(-ROWS[l] * (COLS[l] + 1) // TILE), H), f32) for l in LOW] + [DMA((G,))] * 2,
        compiler_params=pltpu.CompilerParams(vmem_limit_bytes=62 * MIB),
    )(*ins)


def flip(a):
    return jnp.swapaxes(a, 1, 2)


def solution(mesh):
    n_dev = mesh.shape['sp']

    def body(p3, p4, p5, p6, p7, fuse_two, fuse_three, dw_filter, pw_weight, bn_scale, bn_bias):
        two, three = fuse_two.T, fuse_three
        qs = [flip(a) for a in (p5, p6, p7)]
        wts = (jnp.transpose(dw_filter, (1, 2, 0, 3)), pw_weight, bn_scale, bn_bias)
        t4, t5, t6, h3, *xs = call_top_down(n_dev, two, three, p3, p4, qs, wts)
        out3, d4, h4 = call_fine(two, three, p3, h3, t4, wts)
        outs = call_bottom_up(n_dev, two, three, p4, qs, xs, (t4, t5, t6), d4, h4, wts)
        out4, *rest = call_finish(outs)
        return out3, out4, *[flip(a) for a in rest]

    band_spec = P('dp', 'sp')
    whole = P()
    return jax.shard_map(body, mesh=mesh, in_specs=(band_spec,) * 5 + (whole,) * 6, out_specs=(band_spec,) * 5, check_vma=False)
```

profile of v0, /device:TPU:11, one launch (start us, length us, event | category | flops | bytes accessed | tf_op | source)
XLA Modules:
  0.0 170.5 jit_solution(6413358802143683742)
XLA Ops:
  0.6 50.1 %shard_map.146 = (bf16[16,18,40,256]{3,2,1,0:T(8,128)(2,1)}, bf16[16,10,20,256]{3,2,1,0:T(8,128)(2,1)}, bf16[16,6,10,256]{3,2,1,0:T(8,128)(2,1)}, bf16[16,2,80,2...) custom-call(f32[2,5]{1,0:T(2,128)} %bitcast.17, ...), custom_call_target="tpu_custom_call" | custom-call | tf_op jit(solution)/shard_map/pallas_call | solution.py:368
  50.7 60.5 %shard_map.147 = (bf16[16,32,80,256]{3,2,1,0:T(8,128)(2,1)}, bf16[16,16,40,256]{3,2,1,0:T(8,128)(2,1)}, bf16[16,1,40,256]{3,2,1,0:T(8,128)(2,1)}) custom-call(f32[2,5]{1,0:T(2,128)} %bitcast.18, f32[3,3]{1,0:T(4,128)} %refs_1_.3, bf16[16,32,80,256]{3,2,1,0:T(8,128)(2,1)} %p_ref.1, bf16[16,2,80,256]{3,2,1,0:T(8,128)(2,1)} %get-tuple-element.24.ph_ref, ...), custom_call_target="tpu_custom_call" | custom-call | tf_op jit(solution)/shard_map/pallas_call | solution.py:501
  111.3 52.3 %shard_map.148 = (bf16[16,16,40,256]{3,2,1,0:T(8,128)(2,1)}, bf16[16,8,20,256]{3,2,1,0:T(8,128)(2,1)}, bf16[16,4,10,256]{3,2,1,0:T(8,128)(2,1)}, bf16[16,2,5,256]{3,2,1,0:T(8,128)(2,1)}) custom-call(f32[2,5]{1,0:T(2,128)} %bitcast.19, f32[3,3]{1,0:T(4,128)} %refs_1_.3, bf16[16,16,40,256]{3,2,1,0:T(8,128)(2,1)} %refs_2_.3, bf16[16,20,8,256]{3,2,1,0:T(8,128)(2,1)} %bitcast.9, ...), custom_call_target="tpu_custom_call" | custom-call | tf_op jit(solution)/shard_map/pallas_call | solution.py:725
  163.6 7.0 %shard_map.149 = (bf16[16,16,40,256]{3,2,1,0:T(8,128)(2,1)}, bf16[16,20,8,256]{3,2,1,0:T(8,128)(2,1)}, bf16[16,10,4,256]{3,2,1,0:T(4,128)(2,1)}, bf16[16,5,2,256]{3,2,1,0:T(2,128)(2,1)}) custom-call(bf16[16,16,40,256]{3,2,1,0:T(8,128)(2,1)} %get-tuple-element.35.i4, bf16[16,8,20,256]{3,2,1,0:T(8,128)(2,1)} %get-tuple-element.36.i5, ...), custom_call_target="tpu_custom_call" | custom-call | tf_op jit(solution)/shard_map/pallas_call | solution.py:765
where the time goes:
time: 171 us
  Pallas kernels  170 us (99%)
    pallas_call x1, Pallas kernels, call_fine(): pl.pallas_call(fine, grid=(B + 1,), out_shape=[struct(s) for s in outs],...  60.5 us
    pallas_call x1, Pallas kernels, call_bottom_up(): pl.pallas_call(functools.partial(bottom_up, n_dev=n_dev), out_shape=[stru...  52.3 us
    pallas_call x1, Pallas kernels, call_top_down(): pl.pallas_call(functools.partial(top_down, n_dev=n_dev), out_shape=[struc...  50.1 us
    pallas_call x1, Pallas kernels, call_finish(): pl.pallas_call(finish, out_shape=[struct(shape(4, ROWS[4]))] + [struct(fl...  6.97 us

commit v1 on v0

--- a/solution.py
+++ b/solution.py
@@ -10,15 +10,17 @@
 f32, bf16 = jnp.float32, jnp.bfloat16
 FUSE_EPS = 1e-4
 B, C, H = 16, 256, 128
-G = N = 4
+G, N = 4, 4
 LV = (4, 5, 6, 7)
 LOW = LV[1:]
 TOP, END = 4, 7
 TWO, THREE = range(2), range(3)
+ROW0, ROW1 = pl.ds(0, 1), pl.ds(1, 1)
 ROWS = {3: 32, 4: 16, 5: 8, 6: 4, 7: 2}
 COLS = {3: 80, 4: 40, 5: 20, 6: 10, 7: 5}
 PADC = {3: 80, 4: 40, 5: 24, 6: 16, 7: 8}
-TILE = 8
+TILE = CHUNKS = 8
+TWO_N = B // CHUNKS
 MESH = pl.DeviceIdType.MESH
 NEG = -jnp.inf
 MIB = 2 ** 20
@@ -29,6 +31,10 @@
         fn(g)
         return g
     lax.fori_loop(0, G, body, G)
+
+
+def prev(t):
+    return jnp.maximum(t - 1, 0)
 
 
 def loop(n, unroll=1):
@@ -107,16 +113,41 @@
     return join(out).astype(bf16)
 
 
-def conv_rows(S, D, rows, level, k, wts, put):
+def lagged(level, k, n, nq, step, S, D, wts, before, put, after):
     DW, pw_ref, sc_ref, bi_ref = wts
     W, wp = COLS[level], PADC[level]
-    for i, (ib, o) in enumerate(rows):
-        D[i * wp:i * wp + W, :] = conv_row(S, ib, o, W, DW, k)
+    rows = [(ib, y) for ib in range(S.shape[0]) for y in range(step)]
     m = len(rows) * wp
-    r = jnp.dot(D[:m], pw_ref[k], preferred_element_type=f32)
-    r = (r * sc_ref[k:k + 1] + bi_ref[k:k + 1]).astype(bf16)
-    for i, (ib, o) in enumerate(rows):
-        put(ib, o, r[i * wp:i * wp + W])
+
+    def point(t):
+        i, q = t // nq, t % nq
+        r = jnp.dot(D[t % 2, :m], pw_ref[k], preferred_element_type=f32)
+        r = (r * sc_ref[k:k + 1] + bi_ref[k:k + 1]).astype(bf16)
+        for x, (ib, y) in enumerate(rows):
+            put(i, ib, q * step + y, r[x * wp:x * wp + W])
+
+    def chunk(i, q):
+        t = i * nq + q
+        point(prev(t))
+        for x, (ib, y) in enumerate(rows):
+            D[t % 2, x * wp:x * wp + W, :] = conv_row(S, ib, q * step + y, W, DW, k)
+
+    @loop(n)
+    def _(i):
+        before(i)
+        if nq == 1:
+            chunk(i, 0)
+        else:
+            @loop(nq)
+            def _(q):
+                chunk(i, q)
+        if after is not None:
+            @pl.when(i > 0)
+            def _():
+                after(i - 1)
+    point(n * nq - 1)
+    if after is not None:
+        after(n - 1)
 
 
 def hmax(PV, v, W):
@@ -128,25 +159,48 @@
     return join(out).astype(bf16)
 
 
-def barrier_signal(me, last):
+def links(me, last, relay):
+    lo, hi = last // 2, last // 2 + 1
+    pairs = [(me > 0, me - 1), (me < last, me + 1)]
+    if relay:
+        for a, b in ((lo, last), (last, hi), (hi, 0), (0, lo)):
+            pairs += [(me == a, b), (me == b, a)]
+    return pairs
+
+
+def images(fn):
+    @loop(B // len(TWO))
+    def _(i):
+        for d in TWO:
+            fn(len(TWO) * i + d, d)
+
+
+def rows_first(l, src, dst, off, F):
+    W, R, st = COLS[l], ROWS[l], COLS[l] + 1
+
+    @images
+    def _(b, d):
+        for w in range(W):
+            for c, v in enumerate(halves(src[b, w].astype(f32))):
+                F[d, c, pl.ds(w, R, stride=st), :] = v
+        for r in range(R):
+            dst[b, off + r] = join([F[d, c, r * st:r * st + W, :] for c in TWO]).astype(bf16)
+
+
+def barrier_signal(me, last, relay=False):
     sem = pltpu.get_barrier_semaphore()
-    for cond, d in ((me > 0, -1), (me < last, 1)):
+    for cond, peer in links(me, last, relay):
         @pl.when(cond)
+        def _(peer=peer):
+            pl.semaphore_signal(sem, inc=1, device_id={'sp': peer}, device_id_type=MESH)
+
+
+def barrier_wait(me, last, relay=False):
+    sem = pltpu.get_barrier_semaphore()
+    for d in range(last + 1):
+        @pl.when(me == d)
         def _(d=d):
-            pl.semaphore_signal(sem, inc=1, device_id={'sp': me + d}, device_id_type=MESH)
-
-
-def barrier_wait(me, last):
-    sem = pltpu.get_barrier_semaphore()
-    inner = (me > 0) & (me < last)
-
-    @pl.when(inner)
-    def _():
-        pl.semaphore_wait(sem, 2)
-
-    @pl.when(jnp.logical_not(inner))
-    def _():
-        pl.semaphore_wait(sem, 1)
+            pl.semaphore_wait(sem, sum(bool(c) for c, _ in links(d, last, relay)))
 
 
 def remote(src, dst, ss, rs, dev):
@@ -163,6 +217,10 @@
 
 def vm(s, t=bf16):
     return pltpu.VMEM(s, t)
+
+
+def flip_buffer(l):
+    return vm((2, 2, TILE * -(-ROWS[l] * (COLS[l] + 1) // TILE), H), f32)
 
 
 DMA = pltpu.SemaphoreType.DMA
@@ -185,7 +243,7 @@
 
 EXT = {4: 2, 5: 2, 6: 2, 7: 1}
 TD = (4, 5, 6)
-SLOTS = {4: 1, 5: 1, 6: 4, 7: 4}
+SLOTS = {4: 1, 5: 1, 6: N, 7: N}
 
 
 def top_down(*refs, n_dev):
@@ -198,7 +256,8 @@
     X = dict(zip(LV, take(4)))
     E, T = dict(zip(LV, take(4))), dict(zip(TD, take(3)))
     S, U, F = dict(zip(TD, take(3))), dict(zip(TD, take(3))), dict(zip(LOW, take(3)))
-    D, Z, DW, ls, os, xs, s_up, r_up, s_dn, r_dn, s3, r3, zs = take(13)
+    D, Z, RB, DW, ls, os, xs, s_up, r_up, s_dn, r_dn, s3, r3, zs, rr, fs = take(16)
+    lo, hi = (n_dev - 1) // 2, n_dev // 2
     me = lax.axis_index('sp')
     last = n_dev - 1
     wts = (DW, pw_ref, sc_ref, bi_ref)
@@ -221,30 +280,25 @@
         e = EXT[l]
         return remote(src(l, g, ROWS[l] - e), E[l].at[sl(g), pl.ds(0, e)], s_dn.at[l - TOP, g], r_dn.at[l - TOP, g], me + 1)
 
-    up3 = remote(p3.at[:, pl.ds(0, 1)], h3.at[:, pl.ds(1, 1)], s3.at[0], r3.at[0], me - 1)
-    dn3 = remote(p3.at[:, pl.ds(ROWS[3] - 1, 1)], h3.at[:, pl.ds(0, 1)], s3.at[1], r3.at[1], me + 1)
-
-    barrier_signal(me, last)
+    up3 = remote(p3.at[:, ROW0], h3.at[:, ROW1], s3.at[0], r3.at[0], me - 1)
+    dn3 = remote(p3.at[:, pl.ds(ROWS[3] - 1, 1)], h3.at[:, ROW0], s3.at[1], r3.at[1], me + 1)
+
+    to_relay = {lo: remote(dn3.src_ref, RB, s3.at[1], rr, last), hi: remote(up3.src_ref, RB, s3.at[0], rr, 0)}
+    from_relay = {0: remote(RB, h3.at[:, ROW1], fs, r3.at[0], lo), last: remote(RB, h3.at[:, ROW0], fs, r3.at[1], hi)}
+    barrier_signal(me, last, True)
 
     @groups
     def _(g):
         load(g).start()
 
+    barrier_wait(me, last, True)
+    for d, cp in to_relay.items():
+        @pl.when(me == d)
+        def _(cp=cp):
+            cp.start()
+
     for l in FINE_FIRST[:-1]:
-        W, R, st = COLS[l], ROWS[l], COLS[l] + 1
-
-        @loop(B // 2)
-        def _(i):
-            for d in TWO:
-                b = 2 * i + d
-                for w in range(W):
-                    for c, v in enumerate(halves(Q[l][b, w].astype(f32))):
-                        F[l][d, c, pl.ds(w, R, stride=st), :] = v
-                for r in range(R):
-                    E[l][b, EXT[l] + r] = join([F[l][d, c, r * st:r * st + W, :] for c in TWO]).astype(bf16)
-    widen(dw_ref, DW)
-    for l in TD:
-        zero_edges(S[l], COLS[l])
+        rows_first(l, Q[l], E[l], EXT[l], F[l])
     Z[...] = jnp.zeros(Z.shape, bf16)
     edge = [pltpu.make_async_copy(Z, h3.at[:, pl.ds(i, 1)], zs) for i in TWO]
 
@@ -260,15 +314,20 @@
         for l in LV:
             E[l][:, EXT[l] + ROWS[l]:] = jnp.zeros(shape(l, EXT[l]), bf16)
 
-    barrier_wait(me, last)
-    for cond, cp, big in ((me > 0, up, up3), (me < last, dn, dn3)):
+    for cond, cp, big, other in ((me > 0, up, up3, hi), (me < last, dn, dn3, lo)):
         @pl.when(cond)
-        def _(cp=cp, big=big):
+        def _(cp=cp, big=big, other=other):
             @groups
             def _(g):
                 for l in FINE_FIRST:
                     cp(l, g).start()
-            big.start()
+
+            @pl.when(me != other)
+            def _():
+                big.start()
+    widen(dw_ref, DW)
+    for l in TD:
+        zero_edges(S[l], COLS[l])
 
     def node(l, g):
         k = 6 - l
@@ -282,26 +341,22 @@
             for d in TWO:
                 put_s(S[l], ib, 2 * j + d, W, E[l][b, 2 * j + d].astype(f32) * a1 + x)
 
-        @loop(N // nb)
-        def _(i):
+        def before(i):
             b0 = g * N + i * nb
-
-            def put(ib, o, v):
-                T[l][b0 + ib, o] = v
             if l == TOP:
                 @loop((R + 4) // 4)
                 def _(j):
                     for u in TWO:
                         fill(b0, 0, 2 * j + u, u)
-
-                @loop(3)
-                def _(q):
-                    conv_rows(S[l], D, [(0, q * 6 + y) for y in range(6)], l, k, wts, put)
             else:
                 for ib in range(nb):
                     for j in range((R + 4) // 2):
                         fill(b0 + ib, ib, j, (ib + j) % 2)
-                conv_rows(S[l], D, [(ib, o) for ib in range(nb) for o in range(R + 2)], l, k, wts, put)
+
+        def put(i, ib, o, v):
+            T[l][g * N + i * nb + ib, o] = v
+        nq = 3 if l == TOP else 1
+        lagged(l, k, N // nb, nq, (R + 2) // nq, S[l], D, wts, before, put, None)
 
         for cond, o in ((me == 0, 0), (me == last, R + 1)):
             @pl.when(cond)
@@ -332,8 +387,17 @@
             arrive(l, g)
             node(l, g)
             out(l, g).start()
+        for d, cp in from_relay.items():
+            @pl.when((me == d) & (g == 0))
+            def _(d=d, cp=cp):
+                to_relay[hi if d == 0 else lo].wait_recv()
+                cp.start()
     for l in LV:
         xout(l).start()
+    for d, cp in from_relay.items():
+        @pl.when(me == d)
+        def _(cp=cp):
+            cp.wait_send()
 
     for cond, cp, sent, got in ((me > 0, up, up3, dn3), (me < last, dn, dn3, up3)):
         @pl.when(cond)
@@ -362,9 +426,9 @@
     scratch = [vm(shape(l, ROWS[l] + 2 * EXT[l])) for l in LV] + [vm(shape(l, ROWS[l] + 2)) for l in TD]
     scratch += [vm((SLOTS[l], 2, ROWS[l] + 4, PADC[l] + 2 * TILE, H), f32) for l in TD]
     scratch += [vm((2, 2, COLS[l], H), f32) for l in TD]
-    scratch += [vm((2, 2, TILE * -(-ROWS[l] * (COLS[l] + 1) // TILE), H), f32) for l in LOW]
-    scratch += [vm((24 * 16 + TILE, C)), vm(shape(3, 1)), vm((9, TILE, C), f32)]
-    scratch += [DMA((G,)), DMA((3, G)), DMA((4,))] + [DMA((4, G))] * 4 + [DMA((2,))] * 2 + [DMA]
+    scratch += [flip_buffer(l) for l in LOW]
+    scratch += [vm((2, 24 * 16 + TILE, C)), vm(shape(3, 1)), vm(shape(3, 1)), vm((9, TILE, C), f32)]
+    scratch += [DMA((G,)), DMA((3, G)), DMA((4,))] + [DMA((4, G))] * 4 + [DMA((2,))] * 2 + [DMA] * 3
     return pl.pallas_call(
         functools.partial(top_down, n_dev=n_dev),
         out_shape=[struct(shape(l, ROWS[l] + 2)) for l in TD] + [struct(shape(3, 2))] + [struct(shape(l, 1)) for l in LV],
@@ -382,7 +446,7 @@
 K3 = 3 * C
 
 
-def fine(two, three, p_ref, ph_ref, t_ref, dw_ref, pw_ref, sc_ref, bi_ref, o_ref, d_ref, h_ref, S0, S1, U, X0, X1, D0, D1, PV, WD, DW):
+def fine(two, three, p_ref, ph_ref, t_ref, p4_ref, t4_ref, dw_ref, pw_ref, sc_ref, bi_ref, o_ref, d_ref, h_ref, S0, S1, U, X0, X1, D0, D1, PV, WD, DW):
     R, W, RC, WC = R3, W3, RC3, WC3
     Xb, Db = (X0, X1), (D0, D1)
     a1, a2 = coefs(two, three, 3)
@@ -404,18 +468,18 @@
                         WD[c, r0:r0 + H, half(po)] = v.astype(bf16)
 
     def p1(S, tj, rows, u):
-        x = expand(U.at[u], t_ref[0, tj + 1].astype(f32) * a2, WC)
+        x = expand(U.at[u], t_ref[tj + 1].astype(f32) * a2, WC)
         for v, si in rows:
             put_s(S, 0, si, W, v.astype(f32) * a1 + x)
 
     def borders(S):
-        p1(S, -1, [(ph_ref[0, 0], 0)], 0)
-        p1(S, RC, [(ph_ref[0, 1], R + 1)], 1)
+        p1(S, -1, [(ph_ref[0], 0)], 0)
+        p1(S, RC, [(ph_ref[1], R + 1)], 1)
 
     def act(S, k):
         for t in range(PB):
             tj = k * PB + t
-            p1(S, tj, [(p_ref[0, 2 * tj + d], 2 * tj + d + 1) for d in TWO], t % 2)
+            p1(S, tj, [(p_ref[2 * tj + d], 2 * tj + d + 1) for d in TWO], t % 2)
 
     def gather(S, X, k):
         for c in TWO:
@@ -440,7 +504,7 @@
         o = jnp.dot(D[:2 * PB * W], pw_ref[3], preferred_element_type=f32)
         o = (o * sc_ref[3:4] + bi_ref[3:4]).astype(bf16)
         for y in range(2 * PB):
-            o_ref[0, 2 * PB * k + y] = o[y * W:(y + 1) * W]
+            o_ref[2 * PB * k + y] = o[y * W:(y + 1) * W]
 
     def step(Sn, Sp):
         if Sn is not None:
@@ -451,7 +515,7 @@
         def _(kk):
             for u in TWO:
                 k = 2 * kk + u
-                point(Db[1 - u], jnp.maximum(k - 1, 0))
+                point(Db[1 - u], prev(k))
                 conv(Sp, Xb[u], Db[u], k)
                 gather(Sp, Xb[1 - u], jnp.minimum(k + 1, NB - 1))
                 if Sn is not None:
@@ -482,30 +546,33 @@
 
     @pl.when(b > 0)
     def _():
-        h_ref[0, 0] = hmax(PV, o_ref[0, 0], W)
+        h_ref[0] = hmax(PV, o_ref[0], W)
 
         @loop(RC, unroll=2)
         def _(r):
             rn = jnp.minimum(2 * r + 2, R - 1)
-            d_ref[0, r] = hmax(PV, jnp.maximum(jnp.maximum(o_ref[0, 2 * r], o_ref[0, 2 * r + 1]), o_ref[0, rn]), W)
-
-
-def call_fine(two, three, p, ph, t, wts):
-    def block(s, late=False):
-        return pl.BlockSpec((1,) + s[1:], lambda b: (jnp.maximum(b - 1, 0) if late else jnp.minimum(b, B - 1), 0, 0, 0))
+            d_ref[r] = hmax(PV, jnp.maximum(jnp.maximum(o_ref[2 * r], o_ref[2 * r + 1]), o_ref[rn]), W)
+        a = coefs(two, three, TOP)
+        maps = (p4_ref[0], t4_ref[0], d_ref[0])
+        h_ref[1] = swish(sum(x.astype(f32) * y for x, y in zip(maps, a))).astype(bf16)
+
+
+def call_fine(two, three, p, ph, t, p4, wts):
+    def block(s, late=False, row=0):
+        return pl.BlockSpec((None,) + s[1:], lambda b: (prev(b) if late else jnp.minimum(b, B - 1), row, 0, 0))
     full = [pl.BlockSpec(a.shape, lambda b, n=a.ndim: (0,) * n) for a in wts]
-    outs = [shape(3, R3), shape(4, RC3), shape(4, 1)]
+    outs = [shape(3, R3), shape(4, RC3), shape(4, 2)]
     S = vm((1, 2, R3 + 2, W3 + 2 * TILE, H), f32)
     X = vm((2, PB * W3 + TILE, K3))
     D = vm((2 * PB * W3 + TILE, C))
     return pl.pallas_call(
         fine, grid=(B + 1,),
         out_shape=[struct(s) for s in outs],
-        in_specs=[SMEM] * 2 + [block(a.shape) for a in (p, ph, t)] + full,
+        in_specs=[SMEM] * 2 + [block(a.shape) for a in (p, ph, t)] + [block(shape(4, 1), True, r) for r in TWO] + full,
         out_specs=[block(s, True) for s in outs],
         scratch_shapes=[S, S, vm((2, 2, W3, H), f32), X, X, D, D, vm((2, W3 + TILE, H), f32), vm((2, K3, C)), vm((9, TILE, C), f32)],
         compiler_params=pltpu.CompilerParams(vmem_limit_bytes=60 * MIB),
-    )(two, three, p, ph, t, *wts)
+    )(two, three, p, ph, t, p4, t, *wts)
 
 
 def bottom_up(*refs, n_dev):
@@ -529,18 +596,18 @@
 
     def loads(l, g):
         q = sl(g)
-        pairs = [(Xh[l].at[q], Pv[l].at[q, pl.ds(0, 1)])]
+        pairs = [(Xh[l].at[q], Pv[l].at[q, ROW0])]
         if l == TOP:
-            pairs += [(p4.at[q], Pv[4].at[q, pl.ds(1, ROWS[4])]), (d4.at[q], Dv[4].at[q]), (h4.at[q], UP[4].at[q, pl.ds(0, 1)])]
+            pairs += [(p4.at[q], Pv[4].at[q, pl.ds(1, ROWS[4])]), (d4.at[q], Dv[4].at[q]), (h4.at[q], UP[4].at[q])]
         if l < END:
             pairs += [(Th[l].at[q], Tv[l].at[q])]
         return [pltpu.make_async_copy(a, b, ls.at[l - TOP, g, i]) for i, (a, b) in enumerate(pairs)]
 
     def up(l, g):
-        return remote(UP[l].at[sl(g)], UR[l].at[sl(g)], s_up.at[l - TOP, g], r_up.at[l - TOP, g], me - 1)
+        return remote((h4 if l == TOP else UP[l]).at[sl(g)], UR[l].at[sl(g)], s_up.at[l - TOP, g], r_up.at[l - TOP, g], me - 1)
 
     def dn(l, g):
-        return remote(Dv[l].at[sl(g), pl.ds(ROWS[l] - 1, 1)], DR[l].at[sl(g)], s_dn.at[l - TOP, g], r_dn.at[l - TOP, g], me + 1)
+        return remote((d4 if l == TOP else Dv[l]).at[sl(g), pl.ds(ROWS[l] - 1, 1)], DR[l].at[sl(g)], s_dn.at[l - TOP, g], r_dn.at[l - TOP, g], me + 1)
 
     def send(l, g):
         @pl.when(me > 0)
@@ -579,6 +646,11 @@
         for l in LV:
             for c in loads(l, g):
                 c.start()
+    barrier_wait(me, last)
+
+    @groups
+    def _(g):
+        send(4, g)
     widen(dw_ref, DW)
     for l in LV:
         zero_edges(S[l], COLS[l])
@@ -596,30 +668,8 @@
         for l in LV:
             DR[l][...] = jnp.zeros(shape(l, 1), bf16)
 
-    barrier_wait(me, last)
-
-    @groups
-    def _(g):
-        for c in loads(4, g):
-            c.wait()
-
-        @loop(N)
-        def _(i):
-            first(4, g * N + i)
-        send(4, g)
-
     for l in LOW:
-        W, R, st = COLS[l], ROWS[l], COLS[l] + 1
-
-        @loop(B // 2)
-        def _(i):
-            for d in TWO:
-                b = 2 * i + d
-                for w in range(W):
-                    for c, v in enumerate(halves(Ph[l][b, w].astype(f32))):
-                        F[l][d, c, pl.ds(w, R, stride=st), :] = v
-                for r in range(R):
-                    Pv[l][b, 1 + r] = join([F[l][d, c, r * st:r * st + W, :] for c in TWO]).astype(bf16)
+        rows_first(l, Ph[l], Pv[l], 1, F[l])
 
     def node(l, g):
         W, R = COLS[l], ROWS[l]
@@ -657,31 +707,28 @@
             pooled(n - 1, False)
             first(l + 1, b)
 
-        @loop(N // nb)
-        def _(i):
+        def before(i):
             b0 = g * N + i * nb
             for ib in range(nb):
                 borders(b0 + ib, ib)
-
-            def put(ib, o, v):
-                Ov[l][b0 + ib, o] = v
             if l == TOP:
                 @loop((R - 1) // 3)
                 def _(r):
                     for y in THREE:
                         put_s(S[l], 0, 3 * r + y + 1, W, fuse(l, b0, 3 * r + y, Dv[l][b0, 3 * r + y]))
-
-                @loop(R // 4)
-                def _(q):
-                    conv_rows(S[l], D, [(0, q * 4 + y) for y in range(4)], l, l, wts, put)
             else:
                 for ib in range(nb):
                     for r in range(R - 1):
                         put_s(S[l], ib, r + 1, W, fuse(l, b0 + ib, r, Dv[l][b0 + ib, r]))
-                conv_rows(S[l], D, [(ib, o) for ib in range(nb) for o in range(R)], l, l, wts, put)
-            if l < END:
-                for ib in range(nb):
-                    pools(b0 + ib)
+
+        def put(i, ib, o, v):
+            Ov[l][g * N + i * nb + ib, o] = v
+
+        def after(i):
+            for ib in range(nb):
+                pools(g * N + i * nb + ib)
+        nq = 4 if l == TOP else 1
+        lagged(l, l, N // nb, nq, R // nq, S[l], D, wts, before, put, after if l < END else None)
 
     def out(l, g):
         return pltpu.make_async_copy(Ov[l].at[sl(g)], Oh[l].at[sl(g)], os.at[l - TOP, g])
@@ -693,6 +740,9 @@
 
             @pl.when((g >= 0) & (g < G))
             def _(l=l, g=g):
+                if l == TOP:
+                    for c in loads(l, g):
+                        c.wait()
                 if l < END:
                     for c in loads(l + 1, g):
                         c.wait()
@@ -720,8 +770,8 @@
     scratch = [vm(shape(l, ROWS[l] + 1)) for l in LV] + [vm(shape(l, ROWS[l] + 2)) for l in TD]
     scratch += [vm(shape(l, ROWS[l])) for l in LV] * 2 + [vm(shape(l, 2)) for l in LV] * 2 + [vm(shape(l, 1)) for l in LV]
     scratch += [vm((SLOTS[l], 2, ROWS[l] + 2, PADC[l] + 2 * TILE, H), f32) for l in LV] + [vm((2, PADC[l] + TILE, H), f32) for l in TD]
-    scratch += [vm((2, 2, TILE * -(-ROWS[l] * (COLS[l] + 1) // TILE), H), f32) for l in LOW]
-    scratch += [vm((24 * 16 + TILE, C)), vm((9, TILE, C), f32), DMA((4, G, 5))] + [DMA((4, G))] * 5
+    scratch += [flip_buffer(l) for l in LOW]
+    scratch += [vm((2, 24 * 16 + TILE, C)), vm((9, TILE, C), f32), DMA((4, G, 5))] + [DMA((4, G))] * 5
     return pl.pallas_call(
         functools.partial(bottom_up, n_dev=n_dev),
         out_shape=[struct(shape(l, ROWS[l])) for l in LV],
@@ -734,18 +784,22 @@
 
 def finish(i4, i5, i6, i7, o4, o5, o6, o7, buf, F5, F6, F7, si, so):
     def cin(g):
-        return pltpu.make_async_copy(i4.at[pl.ds(g * N, N)], buf.at[pl.ds(g * N, N)], si.at[g])
+        return pltpu.make_async_copy(i4.at[pl.ds(TWO_N * g, TWO_N)], buf.at[pl.ds(TWO_N * g, TWO_N)], si.at[g])
 
     def cout(g):
-        return pltpu.make_async_copy(buf.at[pl.ds(g * N, N)], o4.at[pl.ds(g * N, N)], so.at[g])
-
-    for g in range(G):
+        return pltpu.make_async_copy(buf.at[pl.ds(TWO_N * g, TWO_N)], o4.at[pl.ds(TWO_N * g, TWO_N)], so.at[g])
+
+    @loop(CHUNKS)
+    def _(g):
         cin(g).start()
-    for g, (l, src, dst, F) in enumerate(((6, i6, o6, F6), (7, i7, o7, F7), (5, i5, o5, F5))):
+    for l, src, dst, F in ((6, i6, o6, F6), (7, i7, o7, F7), (5, i5, o5, F5)):
         W, R, st = COLS[l], ROWS[l], COLS[l] + 1
 
-        @loop(B // 2)
+        @loop(CHUNKS)
         def _(i):
+            if l == 5:
+                cin(i).wait()
+                cout(i).start()
             for d in TWO:
                 b = 2 * i + d
                 for r in range(R):
@@ -753,11 +807,9 @@
                         F[d, c, r * st:r * st + W, :] = v
                 for w in range(W):
                     dst[b, w] = join([F[d, c, pl.ds(w, R, stride=st), :] for c in TWO]).astype(bf16)
-        cin(g).wait()
-        cout(g).start()
-    cin(G - 1).wait()
-    cout(G - 1).start()
-    for g in range(G):
+
+    @loop(CHUNKS)
+    def _(g):
         cout(g).wait()
 
 
@@ -767,7 +819,7 @@
         out_shape=[struct(shape(4, ROWS[4]))] + [struct(flipped(l)) for l in LOW],
         in_specs=[ANY] + [VMEM] * 3,
         out_specs=[ANY] + [VMEM] * 3,
-        scratch_shapes=[vm(shape(4, ROWS[4]))] + [vm((2, 2, TILE * -(-ROWS[l] * (COLS[l] + 1) // TILE), H), f32) for l in LOW] + [DMA((G,))] * 2,
+        scratch_shapes=[vm(shape(4, ROWS[4]))] + [flip_buffer(l) for l in LOW] + [DMA((CHUNKS,))] * 2,
         compiler_params=pltpu.CompilerParams(vmem_limit_bytes=62 * MIB),
     )(*ins)
 
@@ -784,7 +836,7 @@
         qs = [flip(a) for a in (p5, p6, p7)]
         wts = (jnp.transpose(dw_filter, (1, 2, 0, 3)), pw_weight, bn_scale, bn_bias)
         t4, t5, t6, h3, *xs = call_top_down(n_dev, two, three, p3, p4, qs, wts)
-        out3, d4, h4 = call_fine(two, three, p3, h3, t4, wts)
+        out3, d4, h4 = call_fine(two, three, p3, h3, t4, p4, wts)
         outs = call_bottom_up(n_dev, two, three, p4, qs, xs, (t4, t5, t6), d4, h4, wts)
         out4, *rest = call_finish(outs)
         return out3, out4, *[flip(a) for a in rest]

time: 171 us -> 160 us (0.936)
  Pallas kernels: 170 us -> 159 us
    pallas_call x1, Pallas kernels: 50.1 us -> 42.4 us  [call_top_down(): pl.pallas_call(functools.partial(top_down, n_dev=n_dev), out_shape=[struc...]
    pallas_call x1, Pallas kernels: 52.3 us -> 48.8 us  [call_bottom_up(): pl.pallas_call(functools.partial(bottom_up, n_dev=n_dev), out_shape=[stru...]
where the time goes in v1:
time: 160 us
  Pallas kernels  159 us (99%)
    pallas_call x1, Pallas kernels, call_fine(): pl.pallas_call(fine, grid=(B + 1,), out_shape=[struct(s) for s in outs],...  60.9 us
    pallas_call x1, Pallas kernels, call_bottom_up(): pl.pallas_call(functools.partial(bottom_up, n_dev=n_dev), out_shape=[stru...  48.8 us
    pallas_call x1, Pallas kernels, call_top_down(): pl.pallas_call(functools.partial(top_down, n_dev=n_dev), out_shape=[struc...  42.4 us
    pallas_call x1, Pallas kernels, call_finish(): pl.pallas_call(finish, out_shape=[struct(shape(4, ROWS[4]))] + [struct(fl...  7.38 us

profile of v1, /device:TPU:11, one launch (start us, length us, event | category | flops | bytes accessed | tf_op | source)
XLA Modules:
  0.0 160.1 jit_solution(11019933540400296310)
XLA Ops:
  0.6 42.4 %shard_map.146 = (bf16[16,18,40,256]{3,2,1,0:T(8,128)(2,1)}, bf16[16,10,20,256]{3,2,1,0:T(8,128)(2,1)}, bf16[16,6,10,256]{3,2,1,0:T(8,128)(2,1)}, bf16[16,2,80,2...) custom-call(f32[2,5]{1,0:T(2,128)} %bitcast.17, ...), custom_call_target="tpu_custom_call" | custom-call | tf_op jit(solution)/shard_map/pallas_call | solution.py:432
  43.0 60.9 %shard_map.147 = (bf16[16,32,80,256]{3,2,1,0:T(8,128)(2,1)}, bf16[16,16,40,256]{3,2,1,0:T(8,128)(2,1)}, bf16[16,2,40,256]{3,2,1,0:T(8,128)(2,1)}) custom-call(f32[2,5]{1,0:T(2,128)} %bitcast.18, f32[3,3]{1,0:T(4,128)} %refs_1_.3, bf16[16,32,80,256]{3,2,1,0:T(8,128)(2,1)} %p_ref.1, bf16[16,2,80,256]{3,2,1,0:T(8,128)(2,1)} %get-tuple-element.24.ph_ref, ...), custom_call_target="tpu_custom_call" | custom-call | tf_op jit(solution)/shard_map/pallas_call | solution.py:568
  103.9 48.8 %shard_map.148 = (bf16[16,16,40,256]{3,2,1,0:T(8,128)(2,1)}, bf16[16,8,20,256]{3,2,1,0:T(8,128)(2,1)}, bf16[16,4,10,256]{3,2,1,0:T(8,128)(2,1)}, bf16[16,2,5,256]{3,2,1,0:T(8,128)(2,1)}) custom-call(f32[2,5]{1,0:T(2,128)} %bitcast.19, f32[3,3]{1,0:T(4,128)} %refs_1_.3, bf16[16,16,40,256]{3,2,1,0:T(8,128)(2,1)} %refs_2_.3, bf16[16,20,8,256]{3,2,1,0:T(8,128)(2,1)} %bitcast.9, ...), custom_call_target="tpu_custom_call" | custom-call | tf_op jit(solution)/shard_map/pallas_call | solution.py:775
  152.7 7.4 %shard_map.149 = (bf16[16,16,40,256]{3,2,1,0:T(8,128)(2,1)}, bf16[16,20,8,256]{3,2,1,0:T(8,128)(2,1)}, bf16[16,10,4,256]{3,2,1,0:T(4,128)(2,1)}, bf16[16,5,2,256]{3,2,1,0:T(2,128)(2,1)}) custom-call(bf16[16,16,40,256]{3,2,1,0:T(8,128)(2,1)} %get-tuple-element.35.i4, bf16[16,8,20,256]{3,2,1,0:T(8,128)(2,1)} %get-tuple-element.36.i5, ...), custom_call_target="tpu_custom_call" | custom-call | tf_op jit(solution)/shard_map/pallas_call | solution.py:817

commit v2 on v1

--- a/solution.py
+++ b/solution.py
@@ -457,7 +457,7 @@
         widen(dw_ref, DW)
         zero_edges(S0, W)
         zero_edges(S1, W)
-        PV[:, W:, :] = jnp.full((2, TILE, H), NEG, f32)
+        PV[..., W:, :] = jnp.full((PB, 2, TILE, H), NEG, f32)
         eye = lax.broadcasted_iota(jnp.int32, (H, H), 0) == lax.broadcasted_iota(jnp.int32, (H, H), 1)
         for c in TWO:
             for kx in THREE:
@@ -509,17 +509,17 @@
     def step(Sn, Sp):
         if Sn is not None:
             borders(Sn)
-        gather(Sp, Xb[0], 0)
-
-        @loop(NB // 2)
-        def _(kk):
-            for u in TWO:
-                k = 2 * kk + u
-                point(Db[1 - u], prev(k))
-                conv(Sp, Xb[u], Db[u], k)
-                gather(Sp, Xb[1 - u], jnp.minimum(k + 1, NB - 1))
-                if Sn is not None:
-                    act(Sn, k)
+        for k in range(NB):
+            u = k % 2
+            conv(Sp, Xb[u], Db[u], k)
+            if k:
+                point(Db[1 - u], k - 1)
+            if k < NB - 1:
+                gather(Sp, Xb[1 - u], k + 1)
+            elif Sn is not None:
+                gather(Sn, Xb[1 - u], 0)
+            if Sn is not None:
+                act(Sn, k)
         point(Db[1], NB - 1)
 
     @pl.when(b == 0)
@@ -529,6 +529,7 @@
         @loop(NB)
         def _(k):
             act(S0, k)
+        gather(S0, X0, 0)
 
     inner = (b > 0) & (b < B)
 
@@ -546,12 +547,14 @@
 
     @pl.when(b > 0)
     def _():
-        h_ref[0] = hmax(PV, o_ref[0], W)
-
-        @loop(RC, unroll=2)
-        def _(r):
-            rn = jnp.minimum(2 * r + 2, R - 1)
-            d_ref[r] = hmax(PV, jnp.maximum(jnp.maximum(o_ref[2 * r], o_ref[2 * r + 1]), o_ref[rn]), W)
+        h_ref[0] = hmax(PV.at[0], o_ref[0], W)
+
+        @loop(RC // PB)
+        def _(q):
+            for y in range(PB):
+                r = q * PB + y
+                rn = jnp.minimum(2 * r + 2, R - 1)
+                d_ref[r] = hmax(PV.at[y], jnp.maximum(jnp.maximum(o_ref[2 * r], o_ref[2 * r + 1]), o_ref[rn]), W)
         a = coefs(two, three, TOP)
         maps = (p4_ref[0], t4_ref[0], d_ref[0])
         h_ref[1] = swish(sum(x.astype(f32) * y for x, y in zip(maps, a))).astype(bf16)
@@ -570,7 +573,7 @@
         out_shape=[struct(s) for s in outs],
         in_specs=[SMEM] * 2 + [block(a.shape) for a in (p, ph, t)] + [block(shape(4, 1), True, r) for r in TWO] + full,
         out_specs=[block(s, True) for s in outs],
-        scratch_shapes=[S, S, vm((2, 2, W3, H), f32), X, X, D, D, vm((2, W3 + TILE, H), f32), vm((2, K3, C)), vm((9, TILE, C), f32)],
+        scratch_shapes=[S, S, vm((2, 2, W3, H), f32), X, X, D, D, vm((PB, 2, W3 + TILE, H), f32), vm((2, K3, C)), vm((9, TILE, C), f32)],
         compiler_params=pltpu.CompilerParams(vmem_limit_bytes=60 * MIB),
     )(two, three, p, ph, t, p4, t, *wts)
 
@@ -733,24 +736,20 @@
     def out(l, g):
         return pltpu.make_async_copy(Ov[l].at[sl(g)], Oh[l].at[sl(g)], os.at[l - TOP, g])
 
-    @loop(G + 3)
-    def _(t):
-        for l in LV:
-            g = t - (l - 4)
-
-            @pl.when((g >= 0) & (g < G))
-            def _(l=l, g=g):
-                if l == TOP:
-                    for c in loads(l, g):
-                        c.wait()
-                if l < END:
-                    for c in loads(l + 1, g):
-                        c.wait()
-                arrive(l, g)
-                node(l, g)
-                if l < END:
-                    send(l + 1, g)
-                out(l, g).start()
+    for l in LV:
+        @groups
+        def _(g):
+            if l == TOP:
+                for c in loads(l, g):
+                    c.wait()
+            if l < END:
+                for c in loads(l + 1, g):
+                    c.wait()
+            arrive(l, g)
+            node(l, g)
+            if l < END:
+                send(l + 1, g)
+            out(l, g).start()
 
     for cond, cp in ((me > 0, up), (me < last, dn)):
         @pl.when(cond)

time: 160 us -> 154 us (0.963)
  Pallas kernels: 159 us -> 153 us
    pallas_call x1, Pallas kernels: 60.9 us -> 56.8 us  [call_fine(): pl.pallas_call(fine, grid=(B + 1,), out_shape=[struct(s) for s in outs],...]
    pallas_call x1, Pallas kernels: 48.8 us -> 46.3 us  [call_bottom_up(): pl.pallas_call(functools.partial(bottom_up, n_dev=n_dev), out_shape=[stru...]
where the time goes in v2:
time: 154 us
  Pallas kernels  153 us (99%)
    pallas_call x1, Pallas kernels, call_fine(): pl.pallas_call(fine, grid=(B + 1,), out_shape=[struct(s) for s in outs],...  56.8 us
    pallas_call x1, Pallas kernels, call_bottom_up(): pl.pallas_call(functools.partial(bottom_up, n_dev=n_dev), out_shape=[stru...  46.3 us
    pallas_call x1, Pallas kernels, call_top_down(): pl.pallas_call(functools.partial(top_down, n_dev=n_dev), out_shape=[struc...  42.4 us
    pallas_call x1, Pallas kernels, call_finish(): pl.pallas_call(finish, out_shape=[struct(shape(4, ROWS[4]))] + [struct(fl...  7.38 us

profile of v2, /device:TPU:11, one launch (start us, length us, event | category | flops | bytes accessed | tf_op | source)
XLA Modules:
  0.0 153.6 jit_solution(13095945590906500681)
XLA Ops:
  0.6 42.4 %shard_map.146 = (bf16[16,18,40,256]{3,2,1,0:T(8,128)(2,1)}, bf16[16,10,20,256]{3,2,1,0:T(8,128)(2,1)}, bf16[16,6,10,256]{3,2,1,0:T(8,128)(2,1)}, bf16[16,2,80,2...) custom-call(f32[2,5]{1,0:T(2,128)} %bitcast.17, ...), custom_call_target="tpu_custom_call" | custom-call | tf_op jit(solution)/shard_map/pallas_call | solution.py:432
  43.0 56.8 %shard_map.147 = (bf16[16,32,80,256]{3,2,1,0:T(8,128)(2,1)}, bf16[16,16,40,256]{3,2,1,0:T(8,128)(2,1)}, bf16[16,2,40,256]{3,2,1,0:T(8,128)(2,1)}) custom-call(f32[2,5]{1,0:T(2,128)} %bitcast.18, f32[3,3]{1,0:T(4,128)} %refs_1_.3, bf16[16,32,80,256]{3,2,1,0:T(8,128)(2,1)} %p_ref.1, bf16[16,2,80,256]{3,2,1,0:T(8,128)(2,1)} %get-tuple-element.24.ph_ref, ...), custom_call_target="tpu_custom_call" | custom-call | tf_op jit(solution)/shard_map/pallas_call | solution.py:571
  99.9 46.3 %shard_map.148 = (bf16[16,16,40,256]{3,2,1,0:T(8,128)(2,1)}, bf16[16,8,20,256]{3,2,1,0:T(8,128)(2,1)}, bf16[16,4,10,256]{3,2,1,0:T(8,128)(2,1)}, bf16[16,2,5,256]{3,2,1,0:T(8,128)(2,1)}) custom-call(f32[2,5]{1,0:T(2,128)} %bitcast.19, f32[3,3]{1,0:T(4,128)} %refs_1_.3, bf16[16,16,40,256]{3,2,1,0:T(8,128)(2,1)} %refs_2_.3, bf16[16,20,8,256]{3,2,1,0:T(8,128)(2,1)} %bitcast.9, ...), custom_call_target="tpu_custom_call" | custom-call | tf_op jit(solution)/shard_map/pallas_call | solution.py:774
  146.2 7.4 %shard_map.149 = (bf16[16,16,40,256]{3,2,1,0:T(8,128)(2,1)}, bf16[16,20,8,256]{3,2,1,0:T(8,128)(2,1)}, bf16[16,10,4,256]{3,2,1,0:T(4,128)(2,1)}, bf16[16,5,2,256]{3,2,1,0:T(2,128)(2,1)}) custom-call(bf16[16,16,40,256]{3,2,1,0:T(8,128)(2,1)} %get-tuple-element.35.i4, bf16[16,8,20,256]{3,2,1,0:T(8,128)(2,1)} %get-tuple-element.36.i5, ...), custom_call_target="tpu_custom_call" | custom-call | tf_op jit(solution)/shard_map/pallas_call | solution.py:816

commit v3 on v2

--- a/solution.py
+++ b/solution.py
@@ -355,7 +355,7 @@
 
         def put(i, ib, o, v):
             T[l][g * N + i * nb + ib, o] = v
-        nq = 3 if l == TOP else 1
+        nq = 2 if l == TOP else 1
         lagged(l, k, N // nb, nq, (R + 2) // nq, S[l], D, wts, before, put, None)
 
         for cond, o in ((me == 0, 0), (me == last, R + 1)):
@@ -715,10 +715,11 @@
             for ib in range(nb):
                 borders(b0 + ib, ib)
             if l == TOP:
-                @loop((R - 1) // 3)
-                def _(r):
-                    for y in THREE:
-                        put_s(S[l], 0, 3 * r + y + 1, W, fuse(l, b0, 3 * r + y, Dv[l][b0, 3 * r + y]))
+                @loop(len(THREE))
+                def _(q):
+                    for y in range(5):
+                        r = 5 * q + y
+                        put_s(S[l], 0, r + 1, W, fuse(l, b0, r, Dv[l][b0, r]))
             else:
                 for ib in range(nb):
                     for r in range(R - 1):
@@ -730,7 +731,7 @@
         def after(i):
             for ib in range(nb):
                 pools(g * N + i * nb + ib)
-        nq = 4 if l == TOP else 1
+        nq = 2 if l == TOP else 1
         lagged(l, l, N // nb, nq, R // nq, S[l], D, wts, before, put, after if l < END else None)
 
     def out(l, g):
@@ -781,31 +782,52 @@
     )(two, three, p4, *qs, *xs, *ts, d4, h4, *wts)
 
 
-def finish(i4, i5, i6, i7, o4, o5, o6, o7, buf, F5, F6, F7, si, so):
+def finish(*refs):
+    take = splitter(refs)
+    src, dst, got, put, F = [dict(zip(LV, take(4))) for _ in range(4)] + [dict(zip(LOW, take(3)))]
+    si, so, ti, to = take(4)
+    top = got[TOP]
+
+    def piece(g):
+        return pl.ds(TWO_N * g, TWO_N)
+
     def cin(g):
-        return pltpu.make_async_copy(i4.at[pl.ds(TWO_N * g, TWO_N)], buf.at[pl.ds(TWO_N * g, TWO_N)], si.at[g])
+        return pltpu.make_async_copy(src[TOP].at[piece(g)], top.at[piece(g)], si.at[g])
 
     def cout(g):
-        return pltpu.make_async_copy(buf.at[pl.ds(TWO_N * g, TWO_N)], o4.at[pl.ds(TWO_N * g, TWO_N)], so.at[g])
+        return pltpu.make_async_copy(top.at[piece(g)], dst[TOP].at[piece(g)], so.at[g])
+
+    def small_in(l):
+        return pltpu.make_async_copy(src[l], got[l], ti.at[l - TOP])
+
+    def small_out(l):
+        return pltpu.make_async_copy(put[l], dst[l], to.at[l - TOP])
+
+    for l in LOW[::-1]:
+        small_in(l).start()
 
     @loop(CHUNKS)
     def _(g):
         cin(g).start()
-    for l, src, dst, F in ((6, i6, o6, F6), (7, i7, o7, F7), (5, i5, o5, F5)):
+    for l in LOW[::-1]:
         W, R, st = COLS[l], ROWS[l], COLS[l] + 1
+        small_in(l).wait()
 
         @loop(CHUNKS)
         def _(i):
-            if l == 5:
+            if l == LOW[0]:
                 cin(i).wait()
                 cout(i).start()
             for d in TWO:
                 b = 2 * i + d
                 for r in range(R):
-                    for c, v in enumerate(halves(src[b, r].astype(f32))):
-                        F[d, c, r * st:r * st + W, :] = v
+                    for c, v in enumerate(halves(got[l][b, r].astype(f32))):
+                        F[l][d, c, r * st:r * st + W, :] = v
                 for w in range(W):
-                    dst[b, w] = join([F[d, c, pl.ds(w, R, stride=st), :] for c in TWO]).astype(bf16)
+                    put[l][b, w] = join([F[l][d, c, pl.ds(w, R, stride=st), :] for c in TWO]).astype(bf16)
+        small_out(l).start()
+    for l in LOW:
+        small_out(l).wait()
 
     @loop(CHUNKS)
     def _(g):
@@ -813,12 +835,14 @@
 
 
 def call_finish(ins):
+    outs = [shape(4, ROWS[4])] + [flipped(l) for l in LOW]
     return pl.pallas_call(
         finish,
-        out_shape=[struct(shape(4, ROWS[4]))] + [struct(flipped(l)) for l in LOW],
-        in_specs=[ANY] + [VMEM] * 3,
-        out_specs=[ANY] + [VMEM] * 3,
-        scratch_shapes=[vm(shape(4, ROWS[4]))] + [flip_buffer(l) for l in LOW] + [DMA((CHUNKS,))] * 2,
+        out_shape=[struct(x) for x in outs],
+        in_specs=[ANY] * 4,
+        out_specs=[ANY] * 4,
+        scratch_shapes=[vm(a.shape) for a in ins] + [vm((TILE, H))] + [vm(x) for x in outs[1:]] + [flip_buffer(l) for l in LOW]
+        + [DMA((CHUNKS,))] * 2 + [DMA((4,))] * 2,
         compiler_params=pltpu.CompilerParams(vmem_limit_bytes=62 * MIB),
     )(*ins)
 

time: 154 us -> 148 us (0.961)
  Pallas kernels: 153 us -> 147 us
    pallas_call x1, Pallas kernels: 46.3 us -> 41.4 us  [call_bottom_up(): pl.pallas_call(functools.partial(bottom_up, n_dev=n_dev), out_shape=[stru...]
where the time goes in v3:
time: 148 us
  Pallas kernels  147 us (99%)
    pallas_call x1, Pallas kernels, call_fine(): pl.pallas_call(fine, grid=(B + 1,), out_shape=[struct(s) for s in outs],...  56.8 us
    pallas_call x1, Pallas kernels, call_top_down(): pl.pallas_call(functools.partial(top_down, n_dev=n_dev), out_shape=[struc...  42.6 us
    pallas_call x1, Pallas kernels, call_bottom_up(): pl.pallas_call(functools.partial(bottom_up, n_dev=n_dev), out_shape=[stru...  41.4 us
    pallas_call x1, Pallas kernels, call_finish(): pl.pallas_call(finish, out_shape=[struct(x) for x in outs], in_specs=[ANY...  6.2 us

profile of v3, /device:TPU:11, one launch (start us, length us, event | category | flops | bytes accessed | tf_op | source)
XLA Modules:
  0.0 147.6 jit_solution(8021693503117132578)
XLA Ops:
  0.6 42.6 %shard_map.146 = (bf16[16,18,40,256]{3,2,1,0:T(8,128)(2,1)}, bf16[16,10,20,256]{3,2,1,0:T(8,128)(2,1)}, bf16[16,6,10,256]{3,2,1,0:T(8,128)(2,1)}, bf16[16,2,80,2...) custom-call(f32[2,5]{1,0:T(2,128)} %bitcast.17, ...), custom_call_target="tpu_custom_call" | custom-call | tf_op jit(solution)/shard_map/pallas_call | solution.py:432
  43.2 56.8 %shard_map.147 = (bf16[16,32,80,256]{3,2,1,0:T(8,128)(2,1)}, bf16[16,16,40,256]{3,2,1,0:T(8,128)(2,1)}, bf16[16,2,40,256]{3,2,1,0:T(8,128)(2,1)}) custom-call(f32[2,5]{1,0:T(2,128)} %bitcast.18, f32[3,3]{1,0:T(4,128)} %refs_1_.3, bf16[16,32,80,256]{3,2,1,0:T(8,128)(2,1)} %p_ref.1, bf16[16,2,80,256]{3,2,1,0:T(8,128)(2,1)} %get-tuple-element.24.ph_ref, ...), custom_call_target="tpu_custom_call" | custom-call | tf_op jit(solution)/shard_map/pallas_call | solution.py:571
  100.1 41.4 %shard_map.148 = (bf16[16,16,40,256]{3,2,1,0:T(8,128)(2,1)}, bf16[16,8,20,256]{3,2,1,0:T(8,128)(2,1)}, bf16[16,4,10,256]{3,2,1,0:T(8,128)(2,1)}, bf16[16,2,5,256]{3,2,1,0:T(8,128)(2,1)}) custom-call(f32[2,5]{1,0:T(2,128)} %bitcast.19, f32[3,3]{1,0:T(4,128)} %refs_1_.3, bf16[16,16,40,256]{3,2,1,0:T(8,128)(2,1)} %refs_2_.3, bf16[16,20,8,256]{3,2,1,0:T(8,128)(2,1)} %bitcast.9, ...), custom_call_target="tpu_custom_call" | custom-call | tf_op jit(solution)/shard_map/pallas_call | solution.py:775
  141.4 6.2 %shard_map.149 = (bf16[16,16,40,256]{3,2,1,0:T(8,128)(2,1)}, bf16[16,20,8,256]{3,2,1,0:T(8,128)(2,1)}, bf16[16,10,4,256]{3,2,1,0:T(4,128)(2,1)}, bf16[16,5,2,256]{3,2,1,0:T(2,128)(2,1)}) custom-call(bf16[16,16,40,256]{3,2,1,0:T(8,128)(2,1)} %get-tuple-element.35.refs_0_, bf16[16,8,20,256]{3,2,1,0:T(8,128)(2,1)} %get-tuple-element.36.refs_1_, ...), custom_call_target="tpu_custom_call" | custom-call | tf_op jit(solution)/shard_map/pallas_call | solution.py:839

commit v4 on v3

--- a/solution.py
+++ b/solution.py
@@ -219,6 +219,10 @@
     return pltpu.VMEM(s, t)
 
 
+def product_rows():
+    return vm((2, 24 * 16 + TILE, C))
+
+
 def flip_buffer(l):
     return vm((2, 2, TILE * -(-ROWS[l] * (COLS[l] + 1) // TILE), H), f32)
 
@@ -241,9 +245,9 @@
     return take
 
 
-EXT = {4: 2, 5: 2, 6: 2, 7: 1}
+EXT = dict(zip(LV, (2, 2, 2, 1)))
 TD = (4, 5, 6)
-SLOTS = {4: 1, 5: 1, 6: N, 7: N}
+SLOTS = dict(zip(LV, (1, 1, N, N)))
 
 
 def top_down(*refs, n_dev):
@@ -296,6 +300,10 @@
         @pl.when(me == d)
         def _(cp=cp):
             cp.start()
+    for cond, cp in ((me > 0, up), (me < last, dn)):
+        @pl.when(cond)
+        def _(cp=cp):
+            cp(TOP, 0).start()
 
     for l in FINE_FIRST[:-1]:
         rows_first(l, Q[l], E[l], EXT[l], F[l])
@@ -319,8 +327,12 @@
         def _(cp=cp, big=big, other=other):
             @groups
             def _(g):
-                for l in FINE_FIRST:
+                for l in FINE_FIRST[:-1]:
                     cp(l, g).start()
+
+                @pl.when(g > 0)
+                def _():
+                    cp(TOP, g).start()
 
             @pl.when(me != other)
             def _():
@@ -427,7 +439,7 @@
     scratch += [vm((SLOTS[l], 2, ROWS[l] + 4, PADC[l] + 2 * TILE, H), f32) for l in TD]
     scratch += [vm((2, 2, COLS[l], H), f32) for l in TD]
     scratch += [flip_buffer(l) for l in LOW]
-    scratch += [vm((2, 24 * 16 + TILE, C)), vm(shape(3, 1)), vm(shape(3, 1)), vm((9, TILE, C), f32)]
+    scratch += [product_rows(), vm(shape(3, 1)), vm(shape(3, 1)), vm((9, TILE, C), f32)]
     scratch += [DMA((G,)), DMA((3, G)), DMA((4,))] + [DMA((4, G))] * 4 + [DMA((2,))] * 2 + [DMA] * 3
     return pl.pallas_call(
         functools.partial(top_down, n_dev=n_dev),
@@ -506,6 +518,13 @@
         for y in range(2 * PB):
             o_ref[2 * PB * k + y] = o[y * W:(y + 1) * W]
 
+    def pool(k):
+        for y in range(PB):
+            r = PB * k - 1 + y
+            if r >= 0:
+                m = jnp.maximum(jnp.maximum(o_ref[2 * r], o_ref[2 * r + 1]), o_ref[2 * r + 2])
+                d_ref[r] = hmax(PV.at[y], m, W)
+
     def step(Sn, Sp):
         if Sn is not None:
             borders(Sn)
@@ -514,6 +533,7 @@
             conv(Sp, Xb[u], Db[u], k)
             if k:
                 point(Db[1 - u], k - 1)
+                pool(k - 1)
             if k < NB - 1:
                 gather(Sp, Xb[1 - u], k + 1)
             elif Sn is not None:
@@ -521,6 +541,8 @@
             if Sn is not None:
                 act(Sn, k)
         point(Db[1], NB - 1)
+        pool(NB - 1)
+        d_ref[RC - 1] = hmax(PV.at[0], jnp.maximum(o_ref[R - 2], o_ref[R - 1]), W)
 
     @pl.when(b == 0)
     def _():
@@ -549,12 +571,6 @@
     def _():
         h_ref[0] = hmax(PV.at[0], o_ref[0], W)
 
-        @loop(RC // PB)
-        def _(q):
-            for y in range(PB):
-                r = q * PB + y
-                rn = jnp.minimum(2 * r + 2, R - 1)
-                d_ref[r] = hmax(PV.at[y], jnp.maximum(jnp.maximum(o_ref[2 * r], o_ref[2 * r + 1]), o_ref[rn]), W)
         a = coefs(two, three, TOP)
         maps = (p4_ref[0], t4_ref[0], d_ref[0])
         h_ref[1] = swish(sum(x.astype(f32) * y for x, y in zip(maps, a))).astype(bf16)
@@ -771,7 +787,7 @@
     scratch += [vm(shape(l, ROWS[l])) for l in LV] * 2 + [vm(shape(l, 2)) for l in LV] * 2 + [vm(shape(l, 1)) for l in LV]
     scratch += [vm((SLOTS[l], 2, ROWS[l] + 2, PADC[l] + 2 * TILE, H), f32) for l in LV] + [vm((2, PADC[l] + TILE, H), f32) for l in TD]
     scratch += [flip_buffer(l) for l in LOW]
-    scratch += [vm((2, 24 * 16 + TILE, C)), vm((9, TILE, C), f32), DMA((4, G, 5))] + [DMA((4, G))] * 5
+    scratch += [product_rows(), vm((9, TILE, C), f32), DMA((4, G, 5))] + [DMA((4, G))] * 5
     return pl.pallas_call(
         functools.partial(bottom_up, n_dev=n_dev),
         out_shape=[struct(shape(l, ROWS[l])) for l in LV],

time: 148 us -> 145 us (0.980)
  Pallas kernels: 147 us -> 145 us
    pallas_call x1, Pallas kernels: 56.8 us -> 55 us  [call_fine(): pl.pallas_call(fine, grid=(B + 1,), out_shape=[struct(s) for s in outs],...]
where the time goes in v4:
time: 145 us
  Pallas kernels  145 us (100%)
    pallas_call x1, Pallas kernels, call_fine(): pl.pallas_call(fine, grid=(B + 1,), out_shape=[struct(s) for s in outs],...  55 us
    pallas_call x1, Pallas kernels, call_top_down(): pl.pallas_call(functools.partial(top_down, n_dev=n_dev), out_shape=[struc...  41.9 us
    pallas_call x1, Pallas kernels, call_bottom_up(): pl.pallas_call(functools.partial(bottom_up, n_dev=n_dev), out_shape=[stru...  41.5 us
    pallas_call x1, Pallas kernels, call_finish(): pl.pallas_call(finish, out_shape=[struct(x) for x in outs], in_specs=[ANY...  6.2 us

profile of v4, /device:TPU:11, one launch (start us, length us, event | category | flops | bytes accessed | tf_op | source)
XLA Modules:
  0.0 145.3 jit_solution(6575692644595806262)
XLA Ops:
  0.6 41.9 %shard_map.146 = (bf16[16,18,40,256]{3,2,1,0:T(8,128)(2,1)}, bf16[16,10,20,256]{3,2,1,0:T(8,128)(2,1)}, bf16[16,6,10,256]{3,2,1,0:T(8,128)(2,1)}, bf16[16,2,80,2...) custom-call(f32[2,5]{1,0:T(2,128)} %bitcast.17, ...), custom_call_target="tpu_custom_call" | custom-call | tf_op jit(solution)/shard_map/pallas_call | solution.py:444
  42.6 55.0 %shard_map.147 = (bf16[16,32,80,256]{3,2,1,0:T(8,128)(2,1)}, bf16[16,16,40,256]{3,2,1,0:T(8,128)(2,1)}, bf16[16,2,40,256]{3,2,1,0:T(8,128)(2,1)}) custom-call(f32[2,5]{1,0:T(2,128)} %bitcast.18, f32[3,3]{1,0:T(4,128)} %refs_1_.3, bf16[16,32,80,256]{3,2,1,0:T(8,128)(2,1)} %p_ref.1, bf16[16,2,80,256]{3,2,1,0:T(8,128)(2,1)} %get-tuple-element.24.ph_ref, ...), custom_call_target="tpu_custom_call" | custom-call | tf_op jit(solution)/shard_map/pallas_call | solution.py:587
  97.6 41.5 %shard_map.148 = (bf16[16,16,40,256]{3,2,1,0:T(8,128)(2,1)}, bf16[16,8,20,256]{3,2,1,0:T(8,128)(2,1)}, bf16[16,4,10,256]{3,2,1,0:T(8,128)(2,1)}, bf16[16,2,5,256]{3,2,1,0:T(8,128)(2,1)}) custom-call(f32[2,5]{1,0:T(2,128)} %bitcast.19, f32[3,3]{1,0:T(4,128)} %refs_1_.3, bf16[16,16,40,256]{3,2,1,0:T(8,128)(2,1)} %refs_2_.3, bf16[16,20,8,256]{3,2,1,0:T(8,128)(2,1)} %bitcast.9, ...), custom_call_target="tpu_custom_call" | custom-call | tf_op jit(solution)/shard_map/pallas_call | solution.py:791
  139.1 6.2 %shard_map.149 = (bf16[16,16,40,256]{3,2,1,0:T(8,128)(2,1)}, bf16[16,20,8,256]{3,2,1,0:T(8,128)(2,1)}, bf16[16,10,4,256]{3,2,1,0:T(4,128)(2,1)}, bf16[16,5,2,256]{3,2,1,0:T(2,128)(2,1)}) custom-call(bf16[16,16,40,256]{3,2,1,0:T(8,128)(2,1)} %get-tuple-element.35.refs_0_, bf16[16,8,20,256]{3,2,1,0:T(8,128)(2,1)} %get-tuple-element.36.refs_1_, ...), custom_call_target="tpu_custom_call" | custom-call | tf_op jit(solution)/shard_map/pallas_call | solution.py:855
